TPU v7x, 32 devices: a whole 2x2x4 slice. The times are simulated.
32 devices in a mesh: rep: 8 (over y, x, core), tp: 4 (over z).
Axes of the slice: x: 2, y: 2, z: 4, core: 2. Of those that a mesh axis runs over, the one named last changes fastest.
Arguments:
- hidden: bfloat16 [512, 8192], P('rep'), may hold values from -6 to 6
- norm_gain: bfloat16 [8192], replicated, may hold values from 0.5 to 1.5
- query_weight_matrix: bfloat16 [8192, 4096], P(None, 'tp'), may hold values from -0.0625 to 0.0625
- key_value_weight: bfloat16 [2, 8192, 1024], P(None, None, 'tp'), may hold values from -0.0625 to 0.0625
- output_weight_matrix: bfloat16 [4096, 8192], P('tp'), may hold values from -0.375 to 0.375
- input_down_factors: bfloat16 [3, 8192, 64], P(None, ('rep', 'tp')), may hold values from -0.0625 to 0.0625
- query_up_factor: bfloat16 [64, 4096], P(None, ('rep', 'tp')), may hold values from -0.75 to 0.75
- key_value_up_factors: bfloat16 [2, 64, 1024], P(None, None, ('rep', 'tp')), may hold values from -0.75 to 0.75
- output_down_factor: bfloat16 [4096, 64], P(('rep', 'tp')), may hold values from -0.375 to 0.375
- output_up_factor: bfloat16 [64, 8192], P(None, ('rep', 'tp')), may hold values from -0.75 to 0.75
- cache_keys: bfloat16 [512, 8, 128, 128], P('rep', 'tp'), may hold values from -360 to 360
- cache_values: bfloat16 [512, 8, 128, 128], P('rep', 'tp'), may hold values from -6 to 6
- lengths: int32 [512], P('rep'), may hold values from 1 to 127
Outputs:
- attn_out: bfloat16 [512, 8192], P('rep', 'tp')
All inputs are finite; a program needn't handle non-finite values.
Results may differ from a plain program's by a relative error of at most 0.03.
Values may be sent and summed in bfloat16 or wider, within the bound.
A program may use at most 128 MiB of HBM per device.

v0:
```python
import math
import jax
import jax.numpy as jnp
from jax import lax
from jax.sharding import PartitionSpec as P

epsilon = 1e-06
rope_base = 1000000.0
adapter_scale = 0.5


def rope_angles(lengths, head_dim):
    half_dim = head_dim // 2
    frequency = rope_base ** (-(jnp.arange(half_dim, dtype=jnp.float32) * 2.0) / head_dim)
    return lengths.astype(jnp.float32)[:, None] * frequency[None, :]


def rotate(vectors, angles):
    half_dim = vectors.shape[-1] // 2
    cosine = jnp.cos(angles)[:, None, :]
    sine_part = jnp.sin(angles)[:, None, :]
    low_half = vectors[..., :half_dim]
    high_half = vectors[..., half_dim:]
    return jnp.concatenate(
        [low_half * cosine - high_half * sine_part, high_half * cosine + low_half * sine_part],
        axis=-1,
    )


def adapted(normed, frozen_matrix, inner_part, up_factor):
    base_part = jnp.dot(normed, frozen_matrix, preferred_element_type=jnp.float32)
    return base_part + adapter_scale * jnp.dot(
        inner_part, up_factor, preferred_element_type=jnp.float32
    )


def attend(query, new_key, new_value, keys, values, lengths):
    score_scale = 1.0 / math.sqrt(keys.shape[-1])
    scores = (
        jnp.einsum(
            "bkgd,bkld->bkgl", query, keys.astype(jnp.float32), precision=lax.Precision.HIGHEST
        )
        * score_scale
    )
    own_score = jnp.sum(query * new_key.astype(jnp.float32)[:, :, None, :], axis=-1) * score_scale
    live_mask = (
        jnp.arange(keys.shape[2], dtype=jnp.int32)[None, None, None, :]
        < lengths[:, None, None, None]
    )
    row_max = jnp.maximum(jnp.max(jnp.where(live_mask, scores, -1e30), axis=-1), own_score)
    weights = jnp.where(live_mask, jnp.exp(scores - row_max[..., None]), 0.0)
    own_weight = jnp.exp(own_score - row_max)
    denom_sum = jnp.sum(weights, axis=-1) + own_weight
    probs = (weights / denom_sum[..., None]).astype(jnp.bfloat16)
    own_prob = (own_weight / denom_sum).astype(jnp.bfloat16)
    context = jnp.einsum("bkgl,bkld->bkgd", probs, values, preferred_element_type=jnp.float32)
    context = (
        context
        + own_prob.astype(jnp.float32)[..., None] * new_value.astype(jnp.float32)[:, :, None, :]
    )
    return context.astype(jnp.bfloat16)


def regroup(factor, tp_count, group):
    count, rank_dim, wide = factor.shape
    return factor.reshape(count, rank_dim, tp_count, group, wide // (tp_count * group))


def settle(factor):
    count, rank_dim, tp_count, group, piece = factor.shape
    return jnp.swapaxes(factor, 2, 3).reshape(count, rank_dim, group * tp_count * piece)


def local(
    hidden,
    norm_gain,
    query_weight_matrix,
    key_value_weight,
    output_weight_matrix,
    input_down_factors,
    query_up_factor,
    key_value_up_factors,
    output_down_factor,
    output_up_factor,
    cache_keys,
    cache_values,
    lengths,
):
    states = hidden.astype(jnp.float32)
    square = jnp.mean(states * states, axis=-1, keepdims=True)
    normed = (states * lax.rsqrt(square + epsilon) * norm_gain.astype(jnp.float32)).astype(
        jnp.bfloat16
    )
    seq_count = hidden.shape[0]
    block_rows = input_down_factors.shape[1]
    rep_count = lax.axis_size("rep")
    tp_count = lax.axis_size("tp")
    tp_index = lax.axis_index("tp")
    own_features = lax.dynamic_slice_in_dim(
        normed.reshape(seq_count, rep_count, tp_count, block_rows), tp_index, 1, 2
    )
    own_features = own_features.reshape(seq_count, rep_count * block_rows)
    partial_inner = jnp.einsum(
        "bd,jdr->jbr",
        own_features,
        lax.all_gather(input_down_factors, "rep", axis=1, tiled=True),
        preferred_element_type=jnp.float32,
    )
    inner = lax.psum(partial_inner.astype(jnp.bfloat16), "tp")
    query_up_rows = query_up_factor[None]
    out_down_rows = jnp.swapaxes(output_down_factor, 0, 1)[None]
    out_up_rows = output_up_factor[None]
    per_rep = (
        lax.all_gather(query_up_rows, "rep", axis=2, tiled=True),
        lax.all_gather(key_value_up_factors, "rep", axis=2, tiled=True),
        lax.all_gather(out_down_rows, "rep", axis=2, tiled=True),
        lax.all_gather(out_up_rows, "rep", axis=2, tiled=True),
    )
    group = rep_count // tp_count
    arrived = (
        lax.all_to_all(
            regroup(per_rep[0], tp_count, group), "tp", split_axis=2, concat_axis=2, tiled=True
        ),
        lax.all_to_all(
            regroup(per_rep[1], tp_count, group), "tp", split_axis=2, concat_axis=2, tiled=True
        ),
        lax.all_to_all(
            regroup(per_rep[2], tp_count, group), "tp", split_axis=2, concat_axis=2, tiled=True
        ),
        lax.all_to_all(
            regroup(per_rep[3], tp_count, group), "tp", split_axis=2, concat_axis=2, tiled=True
        ),
    )
    query_up_local = settle(arrived[0])
    key_value_up_local = settle(arrived[1])
    out_down_local = settle(arrived[2])
    out_up_local = settle(arrived[3])
    kv_local = cache_keys.shape[1]
    head_dim = cache_keys.shape[3]
    angles = rope_angles(lengths, head_dim)
    query = adapted(normed, query_weight_matrix, inner[0], query_up_local[0]).reshape(
        seq_count, -1, head_dim
    )
    query = rotate(query, angles).reshape(seq_count, kv_local, -1, head_dim)
    new_key = adapted(normed, key_value_weight[0], inner[1], key_value_up_local[0]).reshape(
        seq_count, kv_local, head_dim
    )
    new_key = rotate(new_key, angles).astype(jnp.bfloat16)
    new_value = (
        adapted(normed, key_value_weight[1], inner[2], key_value_up_local[1])
        .reshape(seq_count, kv_local, head_dim)
        .astype(jnp.bfloat16)
    )
    context = attend(query, new_key, new_value, cache_keys, cache_values, lengths).reshape(
        seq_count, -1
    )
    partial_middle = jnp.einsum(
        "bh,rh->br", context, out_down_local[0], preferred_element_type=jnp.float32
    )
    middle = lax.psum(partial_middle, "tp").astype(jnp.bfloat16)
    partial_value = jnp.dot(context, output_weight_matrix, preferred_element_type=jnp.float32)
    summed = lax.psum_scatter(
        partial_value.astype(jnp.bfloat16), "tp", scatter_dimension=1, tiled=True
    ).astype(jnp.float32)
    summed = summed + adapter_scale * jnp.dot(
        middle, out_up_local[0], preferred_element_type=jnp.float32
    )
    return summed.astype(jnp.bfloat16)


def solution(mesh):
    return jax.shard_map(
        local,
        mesh=mesh,
        in_specs=(
            P("rep", None),
            P(),
            P(None, "tp"),
            P(None, None, "tp"),
            P("tp", None),
            P(None, ("rep", "tp"), None),
            P(None, ("rep", "tp")),
            P(None, None, ("rep", "tp")),
            P(("rep", "tp"), None),
            P(None, ("rep", "tp")),
            P("rep", "tp", None, None),
            P("rep", "tp", None, None),
            P("rep"),
        ),
        out_specs=P("rep", "tp"),
        check_vma=False,
    )
```

profile of v0, /device:TPU:0, one launch (start us, length us, event | category | flops | bytes accessed | tf_op | source)
XLA Modules:
  0.0 177.4 jit_solution(7634904349694602952)
XLA Ops:
  6.5 10.9 %all_gather.17 = bf16[2,64,256]{1,2,0:T(8,128)(2,1)S(1)} all-gather(bf16[2,64,32]{1,2,0:T(8,128)(2,1)} %param.20), channel_id=1, replica_groups=mesh['rep'=8,'tp'=4] {'rep'}, dimensions={2}, use_global_device_ids=true | all-gather | bytes 73728 | tf_op jit(solution)/shard_map/all_gather | solution.py:115
  17.4 0.8 reshape.203
  18.2 4.9 %all-to-all-start.1 = ((bf16[4,2,4096]{2,1,0:T(2,128)(2,1)}), bf16[4,2,4096]{2,1,0:T(2,128)(2,1)S(1)}, u32[]{:S(2)}, u32[]{:S(2)}) async-start(bf16[4,2,4096]{2,1,0:T(2,128)(2,1)} %reshape.203), calls=%async_computation.1 | async-start | bytes 131072 | tf_op jit(solution)/shard_map/all_to_all | solution.py:124
  23.1 0.7 convert_element_type.82
  23.8 1.5 fusion.8
  25.4 1.5 fusion.10
  26.9 0.8 reshape.182
  27.7 3.0 %fusion.2 = f32[64,256]{1,0:T(8,128)S(1)} fusion(bf16[64,8192]{1,0:T(8,128)(2,1)S(1)} %fusion.10, bf16[2,8192,256]{2,1,0:T(8,128)(2,1)} %param.16), kind=kOutput, calls=%fused_computation.3 | convolution fusion | flops 268435456 | bytes 5308416 | tf_op jit(solution)/shard_map/dot_general | solution.py:31
  30.7 3.0 %fusion = f32[64,256]{1,0:T(8,128)S(1)} fusion(bf16[64,8192]{1,0:T(8,128)(2,1)S(1)} %fusion.10, bf16[2,8192,256]{2,1,0:T(8,128)(2,1)} %param.16), kind=kOutput, calls=%fused_computation.1 | convolution fusion | flops 268435456 | bytes 5308416 | tf_op jit(solution)/shard_map/dot_general | solution.py:31
  33.8 1.5 dynamic-slice_reduce_fusion
  35.3 0.1 reshape.199
  35.5 12.6 %all_gather.15 = bf16[3,2048,64]{1,2,0:T(8,128)(2,1)S(1)} all-gather(bf16[3,256,64]{1,2,0:T(8,128)(2,1)S(1)} %copy-done), channel_id=1, replica_groups=mesh['rep'=8,'tp'=4] {'rep'}, dimensions={1}, use_global_device_ids=true | all-gather | bytes 884736 | tf_op jit(solution)/shard_map/all_gather | solution.py:106
  48.0 0.4 fusion.17
  48.5 0.2 multiply_cosine_fusion
  48.8 8.3 %all-gather = bf16[64,1024]{1,0:T(8,128)(2,1)S(1)} all-gather(bf16[64,128]{1,0:T(8,128)(2,1)S(1)} %copy-done.2), channel_id=2, replica_groups=mesh['rep'=8,'tp'=4] {'rep'}, dimensions={1}, use_global_device_ids=true | all-gather | bytes 147456 | tf_op jit(solution)/shard_map/all_gather | solution.py:114
  57.1 0.7 copy.50
  57.9 19.8 %psum.14 = bf16[3,64,64]{2,1,0:T(8,128)(2,1)S(1)} all-reduce(bf16[3,64,64]{2,1,0:T(8,128)(2,1)S(1)} %fusion.17), channel_id=1, replica_groups=mesh['rep'=8,'tp'=4] {'tp'}, use_global_device_ids=true, to_apply=%region_1.0 | all-reduce | flops 12288 | bytes 49152 | tf_op jit(solution)/shard_map/psum | solution.py:109
  77.7 3.3 %all-to-all-start = ((bf16[1,64,4,2,128]{4,3,1,0,2:T(2,128)(2,1)}), bf16[1,64,4,2,128]{4,3,1,0,2:T(2,128)(2,1)S(1)}, u32[]{:S(2)}, u32[]{:S(2)}) async-start(bf16[1,64,4,2,128]{4,3,1,0,2:T(2,128)(2,1)} %copy.50), calls=%async_computation | async-start | bytes 262144 | tf_op jit(solution)/shard_map/all_to_all | solution.py:121
  81.1 0.2 reduce-scatter.2.cloned.1.call-start
  81.3 0.1 reshape.204
  81.5 0.2 fusion.14
  81.7 0.2 fusion.16
  81.9 0.2 subtract_convert_fusion
  82.2 4.7 %all-to-all-done = bf16[1,64,4,2,128]{4,3,1,0,2:T(2,128)(2,1)S(1)} async-done(((bf16[1,64,4,2,128]{4,3,1,0,2:T(2,128)(2,1)}), bf16[1,64,4,2,128]{4,3,1,0,2:T(2,128)(2,1)S(1)}, u32[]{:S(2)}, u32[]{:S(2)}) %all-to-all-start) | async-done | bytes 131104 | tf_op jit(solution)/shard_map/all_to_all | solution.py:121
  86.9 0.2 copy.51
  87.2 0.2 convolution_multiply_fusion.2
  87.4 8.8 %fusion.11 = f32[8,8,8,128]{3,1,2,0:T(8,128)S(1)} fusion(f32[64,1024]{1,0:T(8,128)S(1)} %convolution_multiply_fusion.2, bf16[64,8192]{1,0:T(8,128)(2,1)S(1)} %fusion.10, bf16[8192,1024]{1,0:T(8,128)(2,1)} %param.15), kind=kOutput, calls=%fused_computation.19 | convolution fusion | flops 1073807360 | bytes 18350080 | tf_op jit(solution)/shard_map/dot_general | solution.py:31
  96.2 0.2 multiply_subtract_fusion
  96.4 0.1 pad_maximum_fusion
  96.6 0.4 fusion.18
  97.1 8.5 %select_reduce_fusion = (f32[64,2,4]{2,1,0:T(2,128)S(1)}, f32[64,2,4,128]{3,2,1,0:T(4,128)S(1)}) fusion(pred[64,128]{1,0:T(8,128)(4,1)S(1)} %iota_compare_fusion, f32[64,2,4,128]{3,2,1,0:T(4,128)S(1)} %bitcast.58, bf16[64,2,128,128]{3,2,1,0:T(8,128)(2,1)} %param.23), kind=kOutput, calls=%fused_computation.34 | convolution fusion | flops 100859392 | bytes 4728832 | tf_op jit(solution)/shard_map/bkgd,bkld->bkgl/dot_general | solution.py:40
  105.7 0.1 copy.56
  105.8 0.4 fusion.19
  106.6 3.5 %fusion.12 = bf16[64,2,4,128]{3,2,1,0:T(4,128)(2,1)S(1)} fusion(bf16[64,2,128,128]{3,2,1,0:T(8,128)(2,1)} %param.24, f32[64,2,4,128]{3,2,1,0:T(4,128)S(1)} %get-tuple-element.16, f32[64,2,128]{2,1,0:T(2,128)S(1)} %reshape.192, f32[64,2,4]{2,1,0:T(2,128)S(1)} %copy.59, f32[64,2,4]{2,1,0:T(2,128)S(1)} %copy.58, f32[64,2,4]{2,1,0:T(2,128)S(1)} %copy.56, ...), kind=kOutput, calls=%fused_computation.20 | convolution fusion | flops 17235968 | bytes 4667392 | tf_op jit(solution)/shard_map/bkgl,bkld->bkgd/dot_general | solution.py:56
  110.2 9.8 %convolution_convert_fusion = bf16[64,8192]{1,0:T(8,128)(2,1)} fusion(bf16[64,1024]{1,0:T(8,128)(2,1)S(1)} %reshape.189, bf16[1024,8192]{1,0:T(8,128)(2,1)} %param.17), kind=kOutput, calls=%fused_computation | convolution fusion | flops 1074266112 | bytes 17956864 | tf_op jit(solution)/shard_map/dot_general | solution.py:161
  120.0 8.2 %all-gather.1 = bf16[64,1024]{1,0:T(8,128)(2,1)S(1)} all-gather(bf16[64,128]{1,0:T(8,128)(2,1)S(1)} %bitcast.66), channel_id=3, replica_groups=mesh['rep'=8,'tp'=4] {'rep'}, dimensions={1}, use_global_device_ids=true | all-gather | bytes 147456 | tf_op jit(solution)/shard_map/all_gather | solution.py:116
  128.2 0.7 copy.61
  129.0 3.3 %all-to-all-start.2 = ((bf16[1,64,4,2,128]{4,3,1,0,2:T(2,128)(2,1)}), bf16[1,64,4,2,128]{4,3,1,0,2:T(2,128)(2,1)S(1)}, u32[]{:S(2)}, u32[]{:S(2)}) async-start(bf16[1,64,4,2,128]{4,3,1,0,2:T(2,128)(2,1)} %copy.61), calls=%async_computation.3 | async-start | bytes 262144 | tf_op jit(solution)/shard_map/all_to_all | solution.py:127
  132.3 9.8 %all-gather.2 = bf16[64,2048]{1,0:T(8,128)(2,1)S(1)} all-gather(bf16[64,256]{1,0:T(8,128)(2,1)S(1)} %copy-done.1), channel_id=4, replica_groups=mesh['rep'=8,'tp'=4] {'rep'}, dimensions={1}, use_global_device_ids=true | all-gather | bytes 294912 | tf_op jit(solution)/shard_map/all_gather | solution.py:117
  142.1 0.2 reshape.191
  142.2 0.9 copy.63
  143.1 5.0 %all-to-all-start.3 = ((bf16[1,64,4,2,256]{4,3,1,0,2:T(2,128)(2,1)}), bf16[1,64,4,2,256]{4,3,1,0,2:T(2,128)(2,1)S(1)}, u32[]{:S(2)}, u32[]{:S(2)}) async-start(bf16[1,64,4,2,256]{4,3,1,0,2:T(2,128)(2,1)} %copy.63), calls=%async_computation.4 | async-start | bytes 524288 | tf_op jit(solution)/shard_map/all_to_all | solution.py:130
  148.2 0.2 copy.62
  148.4 0.2 fusion.29
  148.6 19.5 %psum.15 = bf16[64,64]{1,0:T(8,128)(2,1)S(1)} all-reduce(f32[64,64]{1,0:T(8,128)S(1)} %fusion.29), channel_id=1, replica_groups=mesh['rep'=8,'tp'=4] {'tp'}, use_global_device_ids=true, to_apply=%region_6.7 | all-reduce | flops 4096 | bytes 24576 | tf_op jit(solution)/shard_map/psum | solution.py:160
  168.1 0.3 copy.64
  168.5 0.2 squeeze_reshape.11
  168.7 1.9 %fusion.7 = bf16[64,2048]{1,0:T(8,128)(2,1)} fusion(bf16[64,2048]{1,0:T(8,128)(2,1)S(1)} %squeeze_reshape.11, bf16[64,2048]{1,0:T(8,128)(2,1)} %reduce-scatter.2.cloned.1.call-done, bf16[64,64]{1,0:T(8,128)(2,1)S(1)} %psum.15), kind=kOutput, calls=%fused_computation.11 | convolution fusion | flops 17301504 | bytes 794624 | tf_op jit(solution)/shard_map/dot_general | solution.py:165
  (40 shorter events, 1.3 us)
Async XLA Ops:
  18.2 59.5 %all-to-all-start.1 = ((bf16[4,2,4096]{2,1,0:T(2,128)(2,1)}), bf16[4,2,4096]{2,1,0:T(2,128)(2,1)S(1)}, u32[]{:S(2)}, u32[]{:S(2)}) async-start(bf16[4,2,4096]{2,1,0:T(2,128)(2,1)} %reshape.203), calls=%async_computation.1 | async-start | bytes 131072 | tf_op jit(solution)/shard_map/all_to_all | solution.py:124
  30.7 4.7 %copy-start = (bf16[3,256,64]{1,2,0:T(8,128)(2,1)S(1)}, bf16[3,256,64]{1,2,0:T(8,128)(2,1)}, u32[]{:S(2)}) copy-start(bf16[3,256,64]{1,2,0:T(8,128)(2,1)} %param.18) | copy-start | bytes 294916
  30.7 17.3 %copy-start.4 = (s32[64]{0:T(128)S(1)}, s32[64]{0:T(128)}, u32[]{:S(2)}) copy-start(s32[64]{0:T(128)} %param.25) | copy-start | bytes 772
  30.7 18.0 %copy-start.2 = (bf16[64,128]{1,0:T(8,128)(2,1)S(1)}, bf16[64,128]{1,0:T(8,128)(2,1)}, u32[]{:S(2)}) copy-start(bf16[64,128]{1,0:T(8,128)(2,1)} %param.19) | copy-start | bytes 49156
  77.7 9.2 %all-to-all-start = ((bf16[1,64,4,2,128]{4,3,1,0,2:T(2,128)(2,1)}), bf16[1,64,4,2,128]{4,3,1,0,2:T(2,128)(2,1)S(1)}, u32[]{:S(2)}, u32[]{:S(2)}) async-start(bf16[1,64,4,2,128]{4,3,1,0,2:T(2,128)(2,1)} %copy.50), calls=%async_computation | async-start | bytes 262144 | tf_op jit(solution)/shard_map/all_to_all | solution.py:121
  81.1 87.6 %reduce-scatter.2.cloned.1.call-start = ((), (), s32[]{:S(2)}) async-start(), calls=%async_computation.5 | async-start | bytes 1310720 | tf_op jit(solution)/shard_map/reduce_scatter | solution.py:162
  110.2 9.8 %copy-start.3 = (bf16[128,64]{0,1:T(8,128)(2,1)S(1)}, bf16[128,64]{0,1:T(8,128)(2,1)}, u32[]{:S(2)}) copy-start(bf16[128,64]{0,1:T(8,128)(2,1)} %param.21) | copy-start | bytes 49156
  110.2 22.1 %copy-start.1 = (bf16[64,256]{1,0:T(8,128)(2,1)S(1)}, bf16[64,256]{1,0:T(8,128)(2,1)}, u32[]{:S(2)}) copy-start(bf16[64,256]{1,0:T(8,128)(2,1)} %param.22) | copy-start | bytes 98308
  129.0 14.2 %all-to-all-start.2 = ((bf16[1,64,4,2,128]{4,3,1,0,2:T(2,128)(2,1)}), bf16[1,64,4,2,128]{4,3,1,0,2:T(2,128)(2,1)S(1)}, u32[]{:S(2)}, u32[]{:S(2)}) async-start(bf16[1,64,4,2,128]{4,3,1,0,2:T(2,128)(2,1)} %copy.61), calls=%async_computation.3 | async-start | bytes 262144 | tf_op jit(solution)/shard_map/all_to_all | solution.py:127
  143.1 25.0 %all-to-all-start.3 = ((bf16[1,64,4,2,256]{4,3,1,0,2:T(2,128)(2,1)}), bf16[1,64,4,2,256]{4,3,1,0,2:T(2,128)(2,1)S(1)}, u32[]{:S(2)}, u32[]{:S(2)}) async-start(bf16[1,64,4,2,256]{4,3,1,0,2:T(2,128)(2,1)} %copy.63), calls=%async_computation.4 | async-start | bytes 524288 | tf_op jit(solution)/shard_map/all_to_all | solution.py:130
Sparse Core Ops, SparseCore 0:
  120.1 27.4 reduce-scatter.1
where the time goes:
time: 178 us; the launch traced here: 177 us
  blocking collectives  89 us (50%)
  matrix products  39.5 us (22%)
  starting transfers between devices  16.8 us (9%)
  between operations  13.8 us (8%)
  local copies, waits for them, and re-layouts  7.97 us (4%)
  other arithmetic  5.58 us (3%)
  waiting for transfers between devices  4.78 us (3%)
    psum x1, blocking collectives, local(): inner = lax.psum(partial_inner.astype(jnp.bfloat16), 'tp')  19.8 us
    psum x1, blocking collectives, local(): middle = lax.psum(partial_middle, 'tp').astype(jnp.bfloat16)  19.5 us
    dot_general x3, matrix products, adapted(): jnp.dot(normed, frozen_matrix, preferred_element_type=jnp.float32)  14.8 us
    all_gather x1, blocking collectives, local(): lax.all_gather(input_down_factors, 'rep', axis=1, tiled=True)  12.6 us
    all_gather x1, blocking collectives, local(): lax.all_gather(key_value_up_factors, 'rep', axis=2, tiled=True)  10.9 us
    dot_general x1, matrix products, local(): jnp.dot(context, output_weight_matrix, preferred_element_type=jnp.float32)  9.79 us
    all_gather x1, blocking collectives, local(): lax.all_gather(out_up_rows, 'rep', axis=2, tiled=True)  9.75 us
    dot_general x1, matrix products, attend(): jnp.einsum('bkgd,bkld->bkgl', query, keys.astype(jnp.float32), precision=...  8.5 us
  transfers between devices with their start and end apart: 5, of which 1 were waited for; matrix products, arithmetic and copies ran while one was open for 10% of the time, Pallas kernels for 0%

commit v1 on v0

--- a/solution.py
+++ b/solution.py
@@ -106,7 +106,9 @@
         lax.all_gather(input_down_factors, "rep", axis=1, tiled=True),
         preferred_element_type=jnp.float32,
     )
-    inner = lax.psum(partial_inner.astype(jnp.bfloat16), "tp")
+    own = partial_inner.astype(jnp.bfloat16)
+    parts = lax.all_gather(own, "tp", axis=0, tiled=False)
+    inner = parts.sum(axis=0)
     query_up_rows = query_up_factor[None]
     out_down_rows = jnp.swapaxes(output_down_factor, 0, 1)[None]
     out_up_rows = output_up_factor[None]

time: 178 us -> 174 us (0.978)
  blocking collectives: 89 us -> 83.4 us
    psum x1 -> x0, blocking collectives: 19.8 us -> none  [local(): inner = lax.psum(partial_inner.astype(jnp.bfloat16), 'tp')]
    all_gather x0 -> x1, blocking collectives: none -> 14.2 us  [local(): parts = lax.all_gather(own, 'tp', axis=0, tiled=False)]
where the time goes in v1:
time: 174 us; the launch traced here: 173 us
  blocking collectives  83.4 us (48%)
  matrix products  39.5 us (23%)
  starting transfers between devices  18.1 us (10%)
  between operations  13.8 us (8%)
  local copies, waits for them, and re-layouts  7.96 us (5%)
  other arithmetic  5.62 us (3%)
  waiting for transfers between devices  5.04 us (3%)
    psum x1, blocking collectives, local(): middle = lax.psum(partial_middle, 'tp').astype(jnp.bfloat16)  19.5 us
    dot_general x3, matrix products, adapted(): jnp.dot(normed, frozen_matrix, preferred_element_type=jnp.float32)  14.8 us
    all_gather x1, blocking collectives, local(): parts = lax.all_gather(own, 'tp', axis=0, tiled=False)  14.2 us
    all_gather x1, blocking collectives, local(): lax.all_gather(input_down_factors, 'rep', axis=1, tiled=True)  12.6 us
    all_gather x1, blocking collectives, local(): lax.all_gather(key_value_up_factors, 'rep', axis=2, tiled=True)  10.9 us
    all_gather x1, blocking collectives, local(): lax.all_gather(out_up_rows, 'rep', axis=2, tiled=True)  9.81 us
    dot_general x1, matrix products, local(): jnp.dot(context, output_weight_matrix, preferred_element_type=jnp.float32)  9.79 us
    dot_general x1, matrix products, attend(): jnp.einsum('bkgd,bkld->bkgl', query, keys.astype(jnp.float32), precision=...  8.5 us
  transfers between devices with their start and end apart: 5, of which 1 were waited for; matrix products, arithmetic and copies ran while one was open for 10% of the time, Pallas kernels for 0%

profile of v1, /device:TPU:0, one launch (start us, length us, event | category | flops | bytes accessed | tf_op | source)
XLA Modules:
  0.0 173.4 jit_solution(18155087864442590587)
XLA Ops:
  6.5 10.9 %all_gather.25 = bf16[2,64,256]{1,2,0:T(8,128)(2,1)S(1)} all-gather(bf16[2,64,32]{1,2,0:T(8,128)(2,1)} %param.20), channel_id=1, replica_groups=mesh['rep'=8,'tp'=4] {'rep'}, dimensions={2}, use_global_device_ids=true | all-gather | bytes 73728 | tf_op jit(solution)/shard_map/all_gather | solution.py:117
  17.4 0.8 reshape.204
  18.2 4.9 %all-to-all-start.1 = ((bf16[4,2,4096]{2,1,0:T(2,128)(2,1)}), bf16[4,2,4096]{2,1,0:T(2,128)(2,1)S(1)}, u32[]{:S(2)}, u32[]{:S(2)}) async-start(bf16[4,2,4096]{2,1,0:T(2,128)(2,1)} %reshape.204), calls=%async_computation.1 | async-start | bytes 131072 | tf_op jit(solution)/shard_map/all_to_all | solution.py:126
  23.1 0.7 convert_element_type.84
  23.8 1.5 fusion.8
  25.4 1.5 fusion.10
  26.9 0.8 reshape.182
  27.7 3.0 %fusion.2 = f32[64,256]{1,0:T(8,128)S(1)} fusion(bf16[64,8192]{1,0:T(8,128)(2,1)S(1)} %fusion.10, bf16[2,8192,256]{2,1,0:T(8,128)(2,1)} %param.16), kind=kOutput, calls=%fused_computation.3 | convolution fusion | flops 268435456 | bytes 5308416 | tf_op jit(solution)/shard_map/dot_general | solution.py:31
  30.7 3.0 %fusion = f32[64,256]{1,0:T(8,128)S(1)} fusion(bf16[64,8192]{1,0:T(8,128)(2,1)S(1)} %fusion.10, bf16[2,8192,256]{2,1,0:T(8,128)(2,1)} %param.16), kind=kOutput, calls=%fused_computation.1 | convolution fusion | flops 268435456 | bytes 5308416 | tf_op jit(solution)/shard_map/dot_general | solution.py:31
  33.8 1.5 dynamic-slice_reduce_fusion
  35.3 0.1 reshape.200
  35.5 12.6 %all_gather.21 = bf16[3,2048,64]{1,2,0:T(8,128)(2,1)S(1)} all-gather(bf16[3,256,64]{1,2,0:T(8,128)(2,1)S(1)} %copy-done), channel_id=1, replica_groups=mesh['rep'=8,'tp'=4] {'rep'}, dimensions={1}, use_global_device_ids=true | all-gather | bytes 884736 | tf_op jit(solution)/shard_map/all_gather | solution.py:106
  48.0 0.4 fusion.17
  48.5 0.2 multiply_cosine_fusion
  48.8 8.3 %all-gather.1 = bf16[64,1024]{1,0:T(8,128)(2,1)S(1)} all-gather(bf16[64,128]{1,0:T(8,128)(2,1)S(1)} %copy-done.2), channel_id=3, replica_groups=mesh['rep'=8,'tp'=4] {'rep'}, dimensions={1}, use_global_device_ids=true | all-gather | bytes 147456 | tf_op jit(solution)/shard_map/all_gather | solution.py:116
  57.1 0.7 copy.50
  57.9 14.2 %all-gather = bf16[12,64,64]{2,1,0:T(8,128)(2,1)S(1)} all-gather(bf16[3,64,64]{2,1,0:T(8,128)(2,1)S(1)} %fusion.17), channel_id=2, replica_groups=mesh['rep'=8,'tp'=4] {'tp'}, dimensions={0}, use_global_device_ids=true | all-gather | bytes 122880 | tf_op jit(solution)/shard_map/all_gather | solution.py:110
  72.1 4.8 %all-to-all-start = ((bf16[1,64,4,2,128]{4,3,1,0,2:T(2,128)(2,1)}), bf16[1,64,4,2,128]{4,3,1,0,2:T(2,128)(2,1)S(1)}, u32[]{:S(2)}, u32[]{:S(2)}) async-start(bf16[1,64,4,2,128]{4,3,1,0,2:T(2,128)(2,1)} %copy.50), calls=%async_computation | async-start | bytes 262144 | tf_op jit(solution)/shard_map/all_to_all | solution.py:123
  77.0 0.1 reshape.205
  77.2 0.2 fusion.14
  77.4 0.2 fusion.16
  77.5 0.2 subtract_convert_fusion
  77.9 5.0 %all-to-all-done = bf16[1,64,4,2,128]{4,3,1,0,2:T(2,128)(2,1)S(1)} async-done(((bf16[1,64,4,2,128]{4,3,1,0,2:T(2,128)(2,1)}), bf16[1,64,4,2,128]{4,3,1,0,2:T(2,128)(2,1)S(1)}, u32[]{:S(2)}, u32[]{:S(2)}) %all-to-all-start) | async-done | bytes 131104 | tf_op jit(solution)/shard_map/all_to_all | solution.py:123
  82.9 0.2 copy.51
  83.1 0.2 convolution_multiply_fusion.2
  83.3 8.8 %fusion.11 = f32[8,8,8,128]{3,1,2,0:T(8,128)S(1)} fusion(f32[64,1024]{1,0:T(8,128)S(1)} %convolution_multiply_fusion.2, bf16[64,8192]{1,0:T(8,128)(2,1)S(1)} %fusion.10, bf16[8192,1024]{1,0:T(8,128)(2,1)} %param.15), kind=kOutput, calls=%fused_computation.19 | convolution fusion | flops 1073807360 | bytes 18350080 | tf_op jit(solution)/shard_map/dot_general | solution.py:31
  92.2 0.2 multiply_subtract_fusion
  92.4 0.1 pad_maximum_fusion
  92.5 0.4 fusion.18
  93.0 8.5 %select_reduce_fusion = (f32[64,2,4]{2,1,0:T(2,128)S(1)}, f32[64,2,4,128]{3,2,1,0:T(4,128)S(1)}) fusion(pred[64,128]{1,0:T(8,128)(4,1)S(1)} %iota_compare_fusion, f32[64,2,4,128]{3,2,1,0:T(4,128)S(1)} %bitcast.59, bf16[64,2,128,128]{3,2,1,0:T(8,128)(2,1)} %param.23), kind=kOutput, calls=%fused_computation.34 | convolution fusion | flops 100859392 | bytes 4728832 | tf_op jit(solution)/shard_map/bkgd,bkld->bkgl/dot_general | solution.py:40
  101.6 0.1 copy.56
  101.8 0.4 fusion.19
  102.4 0.1 copy.59
  102.6 3.5 %fusion.12 = bf16[64,2,4,128]{3,2,1,0:T(4,128)(2,1)S(1)} fusion(bf16[64,2,128,128]{3,2,1,0:T(8,128)(2,1)} %param.24, f32[64,2,4,128]{3,2,1,0:T(4,128)S(1)} %get-tuple-element.16, f32[64,2,128]{2,1,0:T(2,128)S(1)} %reshape.192, f32[64,2,4]{2,1,0:T(2,128)S(1)} %copy.59, f32[64,2,4]{2,1,0:T(2,128)S(1)} %copy.58, f32[64,2,4]{2,1,0:T(2,128)S(1)} %copy.56, ...), kind=kOutput, calls=%fused_computation.20 | convolution fusion | flops 17235968 | bytes 4667392 | tf_op jit(solution)/shard_map/bkgl,bkld->bkgd/dot_general | solution.py:56
  106.1 9.8 %convolution_convert_fusion = bf16[64,8192]{1,0:T(8,128)(2,1)} fusion(bf16[64,1024]{1,0:T(8,128)(2,1)S(1)} %reshape.189, bf16[1024,8192]{1,0:T(8,128)(2,1)} %param.17), kind=kOutput, calls=%fused_computation | convolution fusion | flops 1074266112 | bytes 17956864 | tf_op jit(solution)/shard_map/dot_general | solution.py:163
  115.9 8.1 %all-gather.2 = bf16[64,1024]{1,0:T(8,128)(2,1)S(1)} all-gather(bf16[64,128]{1,0:T(8,128)(2,1)S(1)} %bitcast.68), channel_id=4, replica_groups=mesh['rep'=8,'tp'=4] {'rep'}, dimensions={1}, use_global_device_ids=true | all-gather | bytes 147456 | tf_op jit(solution)/shard_map/all_gather | solution.py:118
  124.1 0.7 copy.61
  124.9 3.3 %all-to-all-start.2 = ((bf16[1,64,4,2,128]{4,3,1,0,2:T(2,128)(2,1)}), bf16[1,64,4,2,128]{4,3,1,0,2:T(2,128)(2,1)S(1)}, u32[]{:S(2)}, u32[]{:S(2)}) async-start(bf16[1,64,4,2,128]{4,3,1,0,2:T(2,128)(2,1)} %copy.61), calls=%async_computation.3 | async-start | bytes 262144 | tf_op jit(solution)/shard_map/all_to_all | solution.py:129
  128.2 9.8 %all-gather.3 = bf16[64,2048]{1,0:T(8,128)(2,1)S(1)} all-gather(bf16[64,256]{1,0:T(8,128)(2,1)S(1)} %copy-done.1), channel_id=5, replica_groups=mesh['rep'=8,'tp'=4] {'rep'}, dimensions={1}, use_global_device_ids=true | all-gather | bytes 294912 | tf_op jit(solution)/shard_map/all_gather | solution.py:119
  138.0 0.2 reshape.191
  138.2 0.9 copy.63
  139.1 5.0 %all-to-all-start.3 = ((bf16[1,64,4,2,256]{4,3,1,0,2:T(2,128)(2,1)}), bf16[1,64,4,2,256]{4,3,1,0,2:T(2,128)(2,1)S(1)}, u32[]{:S(2)}, u32[]{:S(2)}) async-start(bf16[1,64,4,2,256]{4,3,1,0,2:T(2,128)(2,1)} %copy.63), calls=%async_computation.4 | async-start | bytes 524288 | tf_op jit(solution)/shard_map/all_to_all | solution.py:132
  144.1 0.2 copy.62
  144.4 0.2 fusion.29
  144.5 19.5 %psum.7 = bf16[64,64]{1,0:T(8,128)(2,1)S(1)} all-reduce(f32[64,64]{1,0:T(8,128)S(1)} %fusion.29), channel_id=1, replica_groups=mesh['rep'=8,'tp'=4] {'tp'}, use_global_device_ids=true, to_apply=%region_6.7 | all-reduce | flops 4096 | bytes 24576 | tf_op jit(solution)/shard_map/psum | solution.py:162
  164.1 0.3 copy.64
  164.4 0.2 squeeze_reshape.11
  164.7 1.9 %fusion.7 = bf16[64,2048]{1,0:T(8,128)(2,1)} fusion(bf16[64,2048]{1,0:T(8,128)(2,1)S(1)} %squeeze_reshape.11, bf16[64,2048]{1,0:T(8,128)(2,1)} %reduce-scatter.2.cloned.1.call-done, bf16[64,64]{1,0:T(8,128)(2,1)S(1)} %psum.7), kind=kOutput, calls=%fused_computation.11 | convolution fusion | flops 17301504 | bytes 794624 | tf_op jit(solution)/shard_map/dot_general | solution.py:167
  (41 shorter events, 1.3 us)
Async XLA Ops:
  18.2 53.9 %all-to-all-start.1 = ((bf16[4,2,4096]{2,1,0:T(2,128)(2,1)}), bf16[4,2,4096]{2,1,0:T(2,128)(2,1)S(1)}, u32[]{:S(2)}, u32[]{:S(2)}) async-start(bf16[4,2,4096]{2,1,0:T(2,128)(2,1)} %reshape.204), calls=%async_computation.1 | async-start | bytes 131072 | tf_op jit(solution)/shard_map/all_to_all | solution.py:126
  30.7 4.7 %copy-start = (bf16[3,256,64]{1,2,0:T(8,128)(2,1)S(1)}, bf16[3,256,64]{1,2,0:T(8,128)(2,1)}, u32[]{:S(2)}) copy-start(bf16[3,256,64]{1,2,0:T(8,128)(2,1)} %param.18) | copy-start | bytes 294916
  30.7 17.3 %copy-start.4 = (s32[64]{0:T(128)S(1)}, s32[64]{0:T(128)}, u32[]{:S(2)}) copy-start(s32[64]{0:T(128)} %param.25) | copy-start | bytes 772
  30.7 18.0 %copy-start.2 = (bf16[64,128]{1,0:T(8,128)(2,1)S(1)}, bf16[64,128]{1,0:T(8,128)(2,1)}, u32[]{:S(2)}) copy-start(bf16[64,128]{1,0:T(8,128)(2,1)} %param.19) | copy-start | bytes 49156
  72.1 10.8 %all-to-all-start = ((bf16[1,64,4,2,128]{4,3,1,0,2:T(2,128)(2,1)}), bf16[1,64,4,2,128]{4,3,1,0,2:T(2,128)(2,1)S(1)}, u32[]{:S(2)}, u32[]{:S(2)}) async-start(bf16[1,64,4,2,128]{4,3,1,0,2:T(2,128)(2,1)} %copy.50), calls=%async_computation | async-start | bytes 262144 | tf_op jit(solution)/shard_map/all_to_all | solution.py:123
  77.0 87.7 %reduce-scatter.2.cloned.1.call-start = ((), (), s32[]{:S(2)}) async-start(), calls=%async_computation.5 | async-start | bytes 1310720 | tf_op jit(solution)/shard_map/reduce_scatter | solution.py:164
  106.1 9.8 %copy-start.3 = (bf16[128,64]{0,1:T(8,128)(2,1)S(1)}, bf16[128,64]{0,1:T(8,128)(2,1)}, u32[]{:S(2)}) copy-start(bf16[128,64]{0,1:T(8,128)(2,1)} %param.21) | copy-start | bytes 49156
  106.1 22.1 %copy-start.1 = (bf16[64,256]{1,0:T(8,128)(2,1)S(1)}, bf16[64,256]{1,0:T(8,128)(2,1)}, u32[]{:S(2)}) copy-start(bf16[64,256]{1,0:T(8,128)(2,1)} %param.22) | copy-start | bytes 98308
  124.9 14.2 %all-to-all-start.2 = ((bf16[1,64,4,2,128]{4,3,1,0,2:T(2,128)(2,1)}), bf16[1,64,4,2,128]{4,3,1,0,2:T(2,128)(2,1)S(1)}, u32[]{:S(2)}, u32[]{:S(2)}) async-start(bf16[1,64,4,2,128]{4,3,1,0,2:T(2,128)(2,1)} %copy.61), calls=%async_computation.3 | async-start | bytes 262144 | tf_op jit(solution)/shard_map/all_to_all | solution.py:129
  139.1 25.0 %all-to-all-start.3 = ((bf16[1,64,4,2,256]{4,3,1,0,2:T(2,128)(2,1)}), bf16[1,64,4,2,256]{4,3,1,0,2:T(2,128)(2,1)S(1)}, u32[]{:S(2)}, u32[]{:S(2)}) async-start(bf16[1,64,4,2,256]{4,3,1,0,2:T(2,128)(2,1)} %copy.63), calls=%async_computation.4 | async-start | bytes 524288 | tf_op jit(solution)/shard_map/all_to_all | solution.py:132
Sparse Core Ops, SparseCore 0:
  116.1 27.4 reduce-scatter.1
